TPU v7x, 256 devices: a whole 4x4x8 slice. The times are simulated.
256 devices in a mesh: tile: 32 (over z_lo, y, core), img: 8 (over x, z_hi).
Axes of the slice: x: 4, y: 4, z: 8 (z_hi: 2, z_lo: 4; z = z_hi * 4 + z_lo), core: 2. Of those that a mesh axis runs over, the one named last changes fastest.
Arguments:
- tower: bfloat16 [8, 64, 128, 256], P('img', 'tile'), may hold values from -6 to 6
- cls_weight: bfloat16 [720, 2304], replicated, may hold values from -0.125 to 0.125
- cls_bias: float32 [720], replicated, may hold values from -5.5 to -3.5
- box_weight: bfloat16 [36, 2304], replicated, may hold values from -0.125 to 0.125
- box_bias: float32 [36], replicated, may hold values from -0.5 to 0.5
- labels: int32 [8, 9, 64, 128], P('img', None, 'tile'), may hold values from -2 to 79, as said below
- target_index: int32 [8, 9, 64, 128], P('img', None, 'tile'), may hold values from 0 to 99
- boxes: float32 [8, 4, 100], P('img'), may hold values from -320 to 1344, as said below
Outputs:
- loss: float32 [], replicated
- cls_weight_grad: float32 [720, 2304], replicated
- cls_bias_grad: float32 [720], replicated
- box_weight_grad: float32 [36, 2304], replicated
- box_bias_grad: float32 [36], replicated
- tower_grad: bfloat16 [8, 64, 128, 256], P('img', 'tile')
Inputs may be any that keep to these rules, and one draw needn't show every extreme that they name: `labels`: -1 marks background and -2 an ignored anchor, other values are classes; every image has at least one anchor with a class. `boxes`: x1 < x2 and y1 < y2 in every box; sides between 8 and 640 pixels.
All inputs are finite; a program needn't handle non-finite values.
Results may differ from a plain program's by a relative error of at most 0.0053.
Values may be sent and summed in bfloat16 or wider, within the bound.
A program may use at most 64 MiB of HBM per device.

v0:
```python
import jax
import jax.numpy as jnp
from jax import lax
from jax.sharding import PartitionSpec as P

CLASSES = 80
ANCHORS = 9
STRIDE = 8
FOCAL_ALPHA = 0.25
NORM_EPS = 1e-06


def padded_2(value, sides, width):
    for axis, dim in sides:
        peers, length = (lax.axis_size(axis), value.shape[dim])
        up = [(i, (i + 1) % peers) for i in range(peers - 1)]
        down = [(j, i) for i, j in up]
        last = lax.slice_in_dim(value, length - width, length, axis=dim)
        initial = lax.slice_in_dim(value, 0, width, axis=dim)
        before = lax.ppermute(last, axis, up)
        after = lax.ppermute(initial, axis, down)
        value = jnp.concatenate([before, value, after], axis=dim)
    return value


def packed_total(arrays, axis):
    vector, at, gathered = (jnp.concatenate([a.reshape(-1) for a in arrays]), 0, [])
    subtotal = lax.psum(vector, axis)
    for a in arrays:
        gathered.append(subtotal[at : at + a.size].reshape(a.shape))
        at += a.size
    return tuple(gathered)


def build_patches(extended):
    rows_here = extended.shape[1] - 2
    columns = extended.shape[2]
    padded = jnp.pad(extended, ((0, 0), (0, 0), (1, 1), (0, 0)))
    pieces = []
    for row_tap in range(3):
        for col_tap in range(3):
            pieces.append(padded[:, row_tap : row_tap + rows_here, col_tap : col_tap + columns, :])
    return jnp.concatenate(pieces, axis=3)


def taps_back(dpatch, rows_lo, rows_out):
    images_here, rows_in, columns, width_all = dpatch.shape
    channels = width_all // 9
    pieces = dpatch.reshape(images_here, rows_in, columns, 9, channels)
    accumulated = jnp.zeros((images_here, rows_in + 2, columns + 2, channels), jnp.float32)
    for row_tap in range(3):
        for col_tap in range(3):
            accumulated = accumulated.at[
                :, row_tap : row_tap + rows_in, col_tap : col_tap + columns, :
            ].add(pieces[:, :, :, row_tap * 3 + col_tap, :])
    return accumulated[:, rows_lo : rows_lo + rows_out, 1 : columns + 1, :]


def head_terms(logits, deltas, labels, target_index, boxes, first_row):
    images_here = labels.shape[0]
    rows_here = labels.shape[2]
    columns = labels.shape[3]
    scores = logits.reshape(ANCHORS, CLASSES, images_here, rows_here, columns)
    assigned = jnp.transpose(labels, (1, 0, 2, 3))
    classes = lax.broadcasted_iota(jnp.int32, (1, CLASSES, 1, 1, 1), 1)
    target = (assigned[:, None] == classes).astype(jnp.float32)
    counted = (assigned >= -1).astype(jnp.float32)[:, None]
    probability = jax.nn.sigmoid(scores)
    hit_term = -FOCAL_ALPHA * (1.0 - probability) * (1.0 - probability) * jax.nn.log_sigmoid(scores)
    miss_term = -(1.0 - FOCAL_ALPHA) * probability * probability * jax.nn.log_sigmoid(-scores)
    focal_sum = jnp.sum(counted * (target * hit_term + (1.0 - target) * miss_term))
    offsets = deltas.reshape(ANCHORS, 4, images_here, rows_here, columns)
    anchor_ids = lax.broadcasted_iota(jnp.int32, (ANCHORS, 1, 1, 1), 0)
    scale_step = (anchor_ids // 3).astype(jnp.float32)
    ratio_step = (anchor_ids % 3 - 1).astype(jnp.float32)
    anchor_base = 4.0 * STRIDE * jnp.exp2(scale_step / 3.0)
    anchor_w = anchor_base * jnp.exp2(-ratio_step / 2.0)
    anchor_h = anchor_base * jnp.exp2(ratio_step / 2.0)
    row_ids = first_row + lax.broadcasted_iota(jnp.int32, (1, 1, rows_here, 1), 2)
    col_ids = lax.broadcasted_iota(jnp.int32, (1, 1, 1, columns), 3)
    centre_y = (row_ids.astype(jnp.float32) + 0.5) * STRIDE
    centre_x = (col_ids.astype(jnp.float32) + 0.5) * STRIDE
    middle_x = centre_x + offsets[:, 0] * anchor_w
    middle_y = centre_y + offsets[:, 1] * anchor_h
    pred_width = anchor_w * jnp.exp(offsets[:, 2])
    pred_height = anchor_h * jnp.exp(offsets[:, 3])
    pred_left = middle_x - 0.5 * pred_width
    pred_right = middle_x + 0.5 * pred_width
    pred_top = middle_y - 0.5 * pred_height
    pred_bottom = middle_y + 0.5 * pred_height
    flat_index = target_index.reshape(images_here, -1)
    picked = jnp.take_along_axis(
        boxes,
        jnp.broadcast_to(flat_index[:, None, :], (images_here, 4, flat_index.shape[1])),
        axis=2,
    )
    picked = jnp.transpose(
        picked.reshape(images_here, 4, ANCHORS, rows_here, columns), (1, 2, 0, 3, 4)
    )
    true_left, true_top, true_right, true_bottom = (picked[0], picked[1], picked[2], picked[3])
    crossing_w = jnp.maximum(
        jnp.minimum(pred_right, true_right) - jnp.maximum(pred_left, true_left), 0.0
    )
    crossing_h = jnp.maximum(
        jnp.minimum(pred_bottom, true_bottom) - jnp.maximum(pred_top, true_top), 0.0
    )
    crossing = crossing_w * crossing_h
    union_area = (
        pred_width * pred_height + (true_right - true_left) * (true_bottom - true_top) - crossing
    )
    outer_w = jnp.maximum(pred_right, true_right) - jnp.minimum(pred_left, true_left)
    outer_h = jnp.maximum(pred_bottom, true_bottom) - jnp.minimum(pred_top, true_top)
    outer_area = outer_w * outer_h
    giou_value = crossing / union_area - (outer_area - union_area) / outer_area
    positive = (assigned >= 0).astype(jnp.float32)
    giou_sum = jnp.sum(positive * (1.0 - giou_value))
    return (focal_sum, giou_sum)


def per_device(tower, cls_weight, cls_bias, box_weight, box_bias, labels, target_index, boxes):
    images_here = tower.shape[0]
    rows_here = tower.shape[1]
    columns = tower.shape[2]
    split_at = cls_weight.shape[0]
    weight_all = jnp.concatenate([cls_weight, box_weight], axis=0)
    bias_all = jnp.concatenate([cls_bias, box_bias])
    extended = padded_2(tower, (("tile", 1),), 1)
    patches = build_patches(extended)
    flat_patches = patches.reshape(-1, patches.shape[3])
    outputs = lax.dot_general(
        weight_all, flat_patches, (((1,), (1,)), ((), ())), preferred_element_type=jnp.float32
    )
    outputs = (outputs + bias_all[:, None]).reshape(
        weight_all.shape[0], images_here, rows_here, columns
    )
    first_row = lax.axis_index("tile") * rows_here

    def loss_pair(scores, offsets):
        return head_terms(scores, offsets, labels, target_index, boxes, first_row)

    loss_terms, pullback = jax.vjp(loss_pair, outputs[:split_at], outputs[split_at:])
    grad_scores, grad_offsets = pullback((jnp.ones((), jnp.float32), jnp.ones((), jnp.float32)))
    focal_local, giou_local = loss_terms
    count_local = jnp.sum((labels >= 0).astype(jnp.float32))
    grad_out = jnp.concatenate([grad_scores, grad_offsets], axis=0)
    grad_low = grad_out.astype(jnp.bfloat16)
    grad_flat = grad_low.reshape(grad_low.shape[0], -1)
    weight_terms = jnp.dot(grad_flat, flat_patches, preferred_element_type=jnp.float32)
    bias_terms = jnp.sum(grad_out, axis=(1, 2, 3))
    grad_rows = padded_2(grad_low, (("tile", 2),), 1)
    dpatch = lax.dot_general(
        grad_rows.reshape(grad_rows.shape[0], -1),
        weight_all,
        (((0,), (0,)), ((), ())),
        preferred_element_type=jnp.float32,
    )
    dpatch = dpatch.reshape(images_here, rows_here + 2, columns, weight_all.shape[1])
    tower_sum = taps_back(dpatch, 2, rows_here)
    tower_grad = tower_sum.astype(jnp.bfloat16)
    entries = weight_all.shape[0] * (weight_all.shape[1] + 1)
    focal_total, giou_total, positives, bias_sum = packed_total(
        (focal_local, giou_local, count_local, bias_terms), ("tile", "img")
    )
    weight_sum = lax.psum(weight_terms, ("tile", "img"))
    squares = jnp.sum(weight_sum * weight_sum) + jnp.sum(bias_sum * bias_sum)
    scale = lax.rsqrt(squares / entries + NORM_EPS)
    weight_norm = weight_sum * scale
    bias_norm = bias_sum * scale
    loss = (focal_total + giou_total) / positives
    return (
        loss,
        weight_norm[:split_at],
        bias_norm[:split_at],
        weight_norm[split_at:],
        bias_norm[split_at:],
        tower_grad,
    )


def solution(mesh):
    placed = (
        P("img", "tile", None, None),
        P(),
        P(),
        P(),
        P(),
        P("img", None, "tile", None),
        P("img", None, "tile", None),
        P("img", None, None),
    )
    return jax.shard_map(
        per_device,
        mesh=mesh,
        in_specs=placed,
        out_specs=(P(), P(), P(), P(), P(), P("img", "tile", None, None)),
        check_vma=False,
    )
```

profile of v0, /device:TPU:2, one launch (start us, length us, event | category | flops | bytes accessed | tf_op | source)
XLA Modules:
  0.0 431.4 jit_solution(16412508561127130968)
XLA Ops:
  7.2 1.5 fusion.90
  8.8 2.4 collective-permute-start
  11.1 1.3 collective-permute-start.1
  15.6 1.3 compare_convert_fusion
  16.9 75.0 %gather_fusion = f32[9216]{0:T(1024)S(1)} fusion(f32[4,100]{1,0:T(4,128)S(1)} %bitcast.249, s32[9216]{0:T(1024)S(1)} %reshape.1606), kind=kCustom, calls=%fused_computation | custom fusion | bytes 147456 | tf_op jit(solution)/shard_map/jvp(jit(take_along_axis))/gather | solution.py:92
  92.0 2.2 constant_dynamic-update-slice_fusion.1
  94.3 3.6 copy.38
  97.8 1.4 and_reduce_fusion
  106.9 1.5 fusion.65
  110.4 10.4 %fusion.82 = (bf16[9,80,1,2,128]{4,3,1,0,2:T(2,128)(2,1)S(1)}, f32[9,80,1,2,128]{4,3,1,0,2:T(2,128)}, f32[]{:T(128)}) fusion(f32[9,80,1,2,128]{4,3,1,0,2:T(2,128)S(1)} %reshape.1582, f32[9,2,128]{2,1,0:T(2,128)S(1)} %copy-done.7, s32[9,2,128]{2,1,0:T(2,128)S(1)} %bitcast.269), kind=kLoop, calls=%fused_computation.207 | loop fusion | flops 12718079 | bytes 1861636 | tf_op jit(solution)/shard_map/convert.4
  120.8 1.4 copy.33
  122.2 4.0 convolution_bitcast_fusion
  126.4 3.8 collective-permute-start.2
  130.2 1.3 collective-permute-start.3
  132.2 2.0 pad_maximum_fusion.4
  134.3 83.6 %psum.14 = f32[759]{0:T(1024)S(1)} all-reduce(f32[759]{0:T(1024)S(1)} %pad_maximum_fusion.4), channel_id=1, replica_groups=mesh['tile'=32,'img'=8] {'tile','img'}, use_global_device_ids=true, to_apply=%region_4.6 | all-reduce | flops 759 | bytes 6072 | tf_op jit(solution)/shard_map/psum | solution.py:28
  221.1 4.1 convolution_bitcast_fusion.1
  225.3 2.1 copy-done.1
  227.4 1.3 fusion.35
  228.7 2.6 scatter-add.31
  231.3 3.0 add_select_fusion
  234.4 2.7 scatter-add.34
  237.1 1.2 fusion.34
  239.4 1.4 scatter-add.36
  241.9 1.4 scatter-add.39
  243.4 1.2 fusion.30
  245.7 1.4 scatter-add.41
  248.2 1.4 scatter-add.44
  250.4 158.2 %all-reduce.8.cloned.1.call-done = f32[756,2304]{1,0:T(8,128)} async-done(((f32[756,2304]{1,0:T(8,128)}), f32[756,2304]{1,0:T(8,128)}) %all-reduce.8.cloned.1.call-update) | async-done | bytes 6967312 | tf_op jit(solution)/shard_map/psum | solution.py:164
  408.5 5.4 %multiply_reduce_fusion = f32[]{:T(128)} fusion(f32[756,2304]{1,0:T(8,128)} %all-reduce.8.cloned.1.call-done), kind=kLoop, calls=%fused_computation.1 | loop fusion | flops 3483647 | bytes 6967300 | tf_op jit(solution)/shard_map/reduce_sum | solution.py:165
  415.3 3.4 broadcast_multiply_fusion
  419.6 3.2 slice.510
  (83 shorter events, 21.7 us)
Async XLA Ops:
  7.2 9.8 %copy-start = (f32[1,4,100]{2,1,0:T(4,128)S(1)}, f32[1,4,100]{2,1,0:T(4,128)}, u32[]{:S(2)}) copy-start(f32[1,4,100]{2,1,0:T(4,128)} %param.34) | copy-start | bytes 4804
  7.2 401.4 %all-reduce.8.cloned.1.call-start = ((), (), s32[]{:S(2)}) async-start(), calls=%async_computation | async-start | bytes 14008320 | tf_op jit(solution)/shard_map/psum | solution.py:164
  8.8 91.8 %collective-permute-start = (bf16[1,1,128,256]{3,2,1,0:T(8,128)(2,1)}, bf16[1,1,128,256]{3,2,1,0:T(8,128)(2,1)}, u32[]{:S(2)}, u32[]{:S(2)}) collective-permute-start(bf16[1,1,128,256]{3,2,1,0:T(8,128)(2,1)} %get-tuple-element.146), channel_id=1, source_target_pairs={{0,8},{8,16},{16,24},{24,32},{32,40},{40,48},{48,56},{56,64},{64,7... | collective-permute-start | bytes 196616 | tf_op jit(solution)/shard_map/ppermute | solution.py:20
  11.1 89.4 %collective-permute-start.1 = (bf16[1,1,128,256]{3,2,1,0:T(8,128)(2,1)}, bf16[1,1,128,256]{3,2,1,0:T(8,128)(2,1)}, u32[]{:S(2)}, u32[]{:S(2)}) collective-permute-start(bf16[1,1,128,256]{3,2,1,0:T(8,128)(2,1)} %get-tuple-element.147), channel_id=1, source_target_pairs={{8,0},{16,8},{24,16},{32,24},{40,32},{48,40},{56,48},{64,56},{72,6... | collective-permute-start | bytes 196616 | tf_op jit(solution)/shard_map/ppermute | solution.py:21
  13.0 3.9 copy-start.8
  92.0 2.3 copy-start.4
  104.4 1.2 copy-start.2
  105.6 4.4 %copy-start.6 = (f32[9]{0:T(128)S(1)}, f32[9]{0:T(128)}, u32[]{:S(2)}) copy-start(f32[9]{0:T(128)} %get-tuple-element.161) | copy-start | bytes 112
  105.6 4.7 %copy-start.5 = (s32[1,9,2,128]{3,2,1,0:T(2,128)S(1)}, s32[1,9,2,128]{3,2,1,0:T(2,128)}, u32[]{:S(2)}) copy-start(s32[1,9,2,128]{3,2,1,0:T(2,128)} %param.32) | copy-start | bytes 27652
  105.6 4.7 %copy-start.7 = (f32[9,2,128]{2,1,0:T(2,128)S(1)}, f32[9,2,128]{2,1,0:T(2,128)}, u32[]{:S(2)}) copy-start(f32[9,2,128]{2,1,0:T(2,128)} %compare_convert_fusion) | copy-start | bytes 27652
  105.7 16.5 %copy-start.3 = (bf16[1,2,128,2304]{3,2,1,0:T(8,128)(2,1)S(1)}, bf16[1,2,128,2304]{3,2,1,0:T(8,128)(2,1)}, u32[]{:S(2)}) copy-start(bf16[1,2,128,2304]{3,2,1,0:T(8,128)(2,1)} %copy-done.2) | copy-start | bytes 3538948
  126.4 94.7 %collective-permute-start.2 = (bf16[756,1,1,128]{0,3,2,1:T(8,128)(2,1)S(1)}, bf16[756,1,1,128]{0,3,2,1:T(8,128)(2,1)S(1)}, u32[]{:S(2)}, u32[]{:S(2)}) collective-permute-start(bf16[756,1,1,128]{0,3,2,1:T(8,128)(2,1)S(1)} %get-tuple-element.144), channel_id=1, source_target_pairs={{0,8},{8,16},{16,24},{24,32},{32,40},{40,48},{48,56},{56,64},{64,7... | collective-permute-start | bytes 580616 | tf_op jit(solution)/shard_map/ppermute | solution.py:20
  130.2 90.9 %collective-permute-start.3 = (bf16[756,1,1,128]{0,3,2,1:T(8,128)(2,1)S(1)}, bf16[756,1,1,128]{0,3,2,1:T(8,128)(2,1)S(1)}, u32[]{:S(2)}, u32[]{:S(2)}) collective-permute-start(bf16[756,1,1,128]{0,3,2,1:T(8,128)(2,1)S(1)} %get-tuple-element.145), channel_id=1, source_target_pairs={{8,0},{16,8},{24,16},{32,24},{40,32},{48,40},{56,48},{64,56},{72,6... | collective-permute-start | bytes 580616 | tf_op jit(solution)/shard_map/ppermute | solution.py:21
  225.2 2.2 copy-start.1
  415.3 7.5 %copy-start.9 = (f32[756]{0:T(1024)}, f32[756]{0:T(1024)S(1)}, u32[]{:S(2)}) copy-start(f32[756]{0:T(1024)S(1)} %slice_multiply_fusion) | copy-start | bytes 9076
Sparse Core Ops, SparseCore 0:
  126.4 282.1 all-reduce.7
where the time goes:
time: 433 us; the launch traced here: 431 us
  waiting for transfers between devices  158 us (36%)
  local copies, waits for them, and re-layouts  107 us (25%)
  blocking collectives  83.6 us (19%)
  other arithmetic  46 us (11%)
  between operations  19 us (4%)
  matrix products  9.24 us (2%)
  starting transfers between devices  8.76 us (2%)
    psum x1, waiting for transfers between devices, per_device(): weight_sum = lax.psum(weight_terms, ('tile', 'img'))  158 us
    psum x1, blocking collectives, packed_total(): subtotal = lax.psum(vector, axis)  83.6 us
    gather x3, local copies, waits for them, and re-layouts, head_terms(): jnp.take_along_axis(boxes, jnp.broadcast_to(flat_index[:, None, :], (imag...  75 us
    another operation x5, other arithmetic  14.9 us
    scatter-add x7, local copies, waits for them, and re-layouts, taps_back(): accumulated = accumulated.at[:, row_tap:row_tap + rows_in, col_tap:col_ta...  11.1 us
  transfers between devices with their start and end apart: 5, of which 1 were waited for; matrix products, arithmetic and copies ran while one was open for 28% of the time, Pallas kernels for 0%

commit v1 on v0

--- a/solution.py
+++ b/solution.py
@@ -25,7 +25,7 @@
 
 def packed_total(arrays, axis):
     vector, at, gathered = (jnp.concatenate([a.reshape(-1) for a in arrays]), 0, [])
-    subtotal = lax.psum(vector, axis)
+    subtotal = jnp.sum(lax.all_gather(vector, axis), axis=0)
     for a in arrays:
         gathered.append(subtotal[at : at + a.size].reshape(a.shape))
         at += a.size

time: 433 us -> 452 us (1.044)
  waiting for transfers between devices: 158 us -> 243 us
  blocking collectives: 83.6 us -> 0 us
  local copies, waits for them, and re-layouts: 107 us -> 119 us
  other arithmetic: 46 us -> 50.6 us
    unnamed x1 -> x2, waiting for transfers between devices: 0.02 us -> 241 us
    psum x1 -> x0, waiting for transfers between devices: 158 us -> none  [per_device(): weight_sum = lax.psum(weight_terms, ('tile', 'img'))]
    psum x1 -> x0, blocking collectives: 83.6 us -> none  [packed_total(): subtotal = lax.psum(vector, axis)]
  transfers between devices with their start and end apart: 5 -> 5, of which waited for: 1 -> 2; matrix products, arithmetic and copies ran while one was open for 28% -> 26% of each run, Pallas kernels for 0% -> 0%
where the time goes in v1:
time: 452 us; the launch traced here: 450 us
  waiting for transfers between devices  243 us (54%)
  local copies, waits for them, and re-layouts  119 us (26%)
  other arithmetic  50.6 us (11%)
  between operations  18.8 us (4%)
  matrix products  10.5 us (2%)
  starting transfers between devices  8.94 us (2%)
    unnamed x2, waiting for transfers between devices  241 us
    gather x3, local copies, waits for them, and re-layouts, head_terms(): jnp.take_along_axis(boxes, jnp.broadcast_to(flat_index[:, None, :], (imag...  75 us
    another operation x5, other arithmetic  15.2 us
    scatter-add x7, local copies, waits for them, and re-layouts, taps_back(): accumulated = accumulated.at[:, row_tap:row_tap + rows_in, col_tap:col_ta...  11.2 us
  transfers between devices with their start and end apart: 5, of which 2 were waited for; matrix products, arithmetic and copies ran while one was open for 26% of the time, Pallas kernels for 0%

profile of v1, /device:TPU:2, one launch (start us, length us, event | category | flops | bytes accessed | tf_op | source)
XLA Modules:
  0.0 450.4 jit_solution(7481260401381997833)
XLA Ops:
  7.2 1.5 fusion.90
  8.8 2.4 collective-permute-start
  14.2 1.3 compare_convert_fusion
  15.6 75.0 %gather_fusion = f32[9216]{0:T(1024)S(1)} fusion(f32[4,100]{1,0:T(4,128)S(1)} %bitcast.249, s32[9216]{0:T(1024)S(1)} %reshape.1606), kind=kCustom, calls=%fused_computation | custom fusion | bytes 147456 | tf_op jit(solution)/shard_map/jvp(jit(take_along_axis))/gather | solution.py:92
  91.3 2.2 constant_dynamic-update-slice_fusion.1
  103.4 2.4 reshape.1582
  105.8 1.6 fusion.65
  112.8 11.4 %fusion.82 = (bf16[9,80,1,2,128]{4,3,1,0,2:T(2,128)(2,1)S(1)}, f32[9,80,1,2,128]{4,3,1,0,2:T(2,128)}, f32[]{:T(128)}) fusion(f32[9,80,1,2,128]{4,3,1,0,2:T(2,128)} %reshape.1582, f32[9,2,128]{2,1,0:T(2,128)} %compare_convert_fusion, s32[9,2,128]{2,1,0:T(2,128)} %bitcast.269), kind=kLoop, calls=%fused_computation.207 | loop fusion | flops 12718079 | bytes 1861636 | tf_op jit(solution)/shard_map/convert.4
  125.0 2.1 copy.33
  127.1 1.3 fusion.25
  128.4 5.4 %convolution_bitcast_fusion = f32[756,2304]{1,0:T(8,128)} fusion(bf16[1,2,128,2304]{3,2,1,0:T(8,128)(2,1)} %copy-done.2, bf16[36,2,128]{2,0,1:T(8,128)(2,1)S(1)} %copy-done.3, bf16[720,2,128]{2,0,1:T(8,128)(2,1)} %bitcast.252), kind=kOutput, calls=%fused_computation.2 | convolution fusion | flops 892588032 | bytes 8534016 | tf_op jit(solution)/shard_map/dot_general | solution.py:148
  134.8 3.4 maximum_dynamic-update-slice_fusion
  138.2 3.6 copy.38
  142.4 1.3 fusion.24
  143.7 3.8 collective-permute-start.2
  147.5 1.5 collective-permute-start.3
  150.3 1.8 collective-permute-done.3
  152.1 4.0 convolution_bitcast_fusion.1
  156.3 2.1 copy-done.1
  158.3 1.4 fusion.35
  159.7 2.7 scatter-add.31
  162.4 3.1 add_select_fusion
  165.5 2.7 scatter-add.34
  170.6 1.4 scatter-add.36
  173.2 1.4 scatter-add.39
  176.9 1.4 scatter-add.41
  179.5 1.4 scatter-add.44
  181.6 240.8 %all-reduce.10.cloned.1.call-done = (f32[194304]{0:T(1024)}, f32[756,2304]{1,0:T(8,128)}) async-done(((f32[194304]{0:T(1024)}, f32[756,2304]{1,0:T(8,128)}), (f32[194304]{0:T(1024)}, f32[756,2304]{1,0:T(8,128)})) %all-reduce.10.cloned.1.call-update) | async-done | bytes 7744528
  422.4 1.9 reshape.1612
  425.6 5.4 %multiply_reduce_fusion = f32[]{:T(128)} fusion(f32[756,2304]{1,0:T(8,128)} %get-tuple-element.123), kind=kLoop, calls=%fused_computation.1 | loop fusion | flops 3483647 | bytes 6967300 | tf_op jit(solution)/shard_map/reduce_sum | solution.py:165
  432.4 3.4 broadcast_multiply_fusion
  436.6 3.2 slice.510
  (81 shorter events, 33.3 us)
Async XLA Ops:
  7.2 8.4 %copy-start = (f32[1,4,100]{2,1,0:T(4,128)S(1)}, f32[1,4,100]{2,1,0:T(4,128)}, u32[]{:S(2)}) copy-start(f32[1,4,100]{2,1,0:T(4,128)} %param.34) | copy-start | bytes 4804
  7.2 415.2 %all-reduce.10.cloned.1.call-start = ((), (), s32[]{:S(2)}) async-start(), calls=%async_computation | async-start | bytes 15564800
  8.8 86.2 %collective-permute-start = (bf16[1,1,128,256]{3,2,1,0:T(8,128)(2,1)}, bf16[1,1,128,256]{3,2,1,0:T(8,128)(2,1)}, u32[]{:S(2)}, u32[]{:S(2)}) collective-permute-start(bf16[1,1,128,256]{3,2,1,0:T(8,128)(2,1)} %get-tuple-element.148), channel_id=1, source_target_pairs={{0,8},{8,16},{16,24},{24,32},{32,40},{40,48},{48,56},{56,64},{64,7... | collective-permute-start | bytes 196616 | tf_op jit(solution)/shard_map/ppermute | solution.py:20
  11.1 83.9 %collective-permute-start.1 = (bf16[1,1,128,256]{3,2,1,0:T(8,128)(2,1)}, bf16[1,1,128,256]{3,2,1,0:T(8,128)(2,1)}, u32[]{:S(2)}, u32[]{:S(2)}) collective-permute-start(bf16[1,1,128,256]{3,2,1,0:T(8,128)(2,1)} %get-tuple-element.149), channel_id=1, source_target_pairs={{8,0},{16,8},{24,16},{32,24},{40,32},{48,40},{56,48},{64,56},{72,6... | collective-permute-start | bytes 196616 | tf_op jit(solution)/shard_map/ppermute | solution.py:21
  90.6 2.9 copy-start.4
  90.6 2.9 copy-start.6
  98.9 1.0 copy-start.2
  112.8 15.6 %copy-start.3 = (bf16[36,2,128]{2,0,1:T(8,128)(2,1)S(1)}, bf16[36,2,128]{2,0,1:T(8,128)(2,1)}, u32[]{:S(2)}) copy-start(bf16[36,2,128]{2,0,1:T(8,128)(2,1)} %copy.37) | copy-start | bytes 55300
  138.2 11.4 %copy-start.7 = (s32[4]{0:T(128)S(1)}, s32[4]{0:T(128)}, u32[]{:S(2)}) copy-start(s32[4]{0:T(128)} %constant.358.clone.1) | copy-start | bytes 52
  143.7 6.6 %collective-permute-start.2 = (bf16[756,1,1,128]{0,3,2,1:T(8,128)(2,1)S(1)}, bf16[756,1,1,128]{0,3,2,1:T(8,128)(2,1)S(1)}, u32[]{:S(2)}, u32[]{:S(2)}) collective-permute-start(bf16[756,1,1,128]{0,3,2,1:T(8,128)(2,1)S(1)} %get-tuple-element.146), channel_id=1, source_target_pairs={{0,8},{8,16},{16,24},{24,32},{32,40},{40,48},{48,56},{56,64},{64,7... | collective-permute-start | bytes 580616 | tf_op jit(solution)/shard_map/ppermute | solution.py:20
  147.5 4.6 %collective-permute-start.3 = (bf16[756,1,1,128]{0,3,2,1:T(8,128)(2,1)S(1)}, bf16[756,1,1,128]{0,3,2,1:T(8,128)(2,1)S(1)}, u32[]{:S(2)}, u32[]{:S(2)}) collective-permute-start(bf16[756,1,1,128]{0,3,2,1:T(8,128)(2,1)S(1)} %get-tuple-element.147), channel_id=1, source_target_pairs={{8,0},{16,8},{24,16},{32,24},{40,32},{48,40},{56,48},{64,56},{72,6... | collective-permute-start | bytes 580616 | tf_op jit(solution)/shard_map/ppermute | solution.py:21
  156.1 2.2 copy-start.1
  435.9 4.0 copy-start.5
Sparse Core Ops, SparseCore 0:
  138.3 284.0 all-reduce.9
